TPU v7x, 32 devices: a whole 2x2x4 slice. The times are simulated.
32 devices in a mesh: row: 4 (over y, core), col: 8 (over z, x).
Axes of the slice: x: 2, y: 2, z: 4, core: 2. Of those that a mesh axis runs over, the one named last changes fastest.
Arguments:
- root_inverse: bfloat16 [2048, 2048], P('col', 'row'), may hold values from -1 to 3, as said below
- lower_panels: bfloat16 [4, 1536, 1024], P(None, 'col', 'row'), may hold values from -0.375 to 0.375
- struct_blocks: int32 [4, 12], replicated, may hold values from 0 to 15, as said below
- struct_count: int32 [4], replicated, may hold values from 1 to 12, 32 in all
- diag_inverse: float32 [4, 1024, 1024], P(None, 'col', 'row'), may hold values from -1 to 3, as said below
Outputs:
- offdiag: bfloat16 [4, 1536, 1024], P(None, 'col', 'row')
- diag_block: float32 [4, 1024, 1024], P(None, 'col', 'row')
Inputs may be any that keep to these rules, and one draw needn't show every extreme that they name: `struct_blocks`: each row holds 12 different block numbers of the top supernode; supernode c uses the first struct_count[c] of them. `struct_count`: the counts sum to 32; the largest equals 12. `root_inverse`: Symmetric, with a dominant diagonal. `diag_inverse`: each supernode's block is symmetric; diagonal entries lie between 0.85 and 2.15, all other entries within 0.13 of zero.
All inputs are finite; a program needn't handle non-finite values.
Results may differ from a plain program's by a relative error of at most 0.0095.
Values may be sent and summed in bfloat16 or wider, within the bound.
A program may use at most 64 MiB of HBM per device.

v0:
```python
import jax
import jax.numpy as jnp
from jax import lax
from jax.sharding import PartitionSpec as P

BLOCK = 128
NSMAX = 12


def body(root_inverse, lower_panels, struct_blocks, struct_count, diag_inverse):
    col_index = lax.axis_index("col")
    root_panel = lax.all_gather(root_inverse, "row", axis=1, tiled=True)
    root_width = root_panel.shape[1]
    block_count = root_width // BLOCK
    own_rows = root_panel.shape[0]
    per_dev = own_rows // BLOCK
    local_packed = lower_panels.shape[1]

    def solve_group(lower_group, block_lists, block_counts, inverse_group):
        group_size = lower_group.shape[0]
        cols_here = lower_group.shape[2]
        gathered = lax.all_gather(lower_group, "col", axis=1, tiled=True)
        packed_total = gathered.shape[1]
        full_mask = jnp.arange(packed_total)[None, :] // BLOCK < block_counts[:, None]
        gathered = gathered * full_mask[:, :, None].astype(jnp.bfloat16)
        in_use = jnp.arange(NSMAX)[None, :] < block_counts[:, None]
        onehot = (
            (block_lists[:, None, :] == jnp.arange(block_count)[None, :, None]) & in_use[:, None, :]
        ).astype(jnp.bfloat16)
        spread = jnp.einsum(
            "gbk,gkic->gbic",
            onehot,
            gathered.reshape(group_size, NSMAX, BLOCK, cols_here),
            preferred_element_type=jnp.float32,
        )
        spread = spread.astype(jnp.bfloat16).reshape(group_size, root_width, cols_here)
        root_part = -jnp.einsum(
            "rw,gwc->grc", root_panel, spread, preferred_element_type=jnp.float32
        )
        packed_index = col_index * local_packed + jnp.arange(local_packed)
        local_mask = packed_index[None, :] // BLOCK < block_counts[:, None]
        own_select = lax.dynamic_slice_in_dim(onehot, col_index * per_dev, per_dev, 1).astype(
            jnp.float32
        )
        selected = jnp.einsum(
            "gjk,gjic->gkic",
            own_select,
            root_part.reshape(group_size, per_dev, BLOCK, cols_here),
            precision=lax.Precision.HIGHEST,
            preferred_element_type=jnp.float32,
        )
        selected = selected.reshape(group_size, packed_total, cols_here)
        offdiag = lax.psum_scatter(
            selected.astype(jnp.bfloat16), "col", scatter_dimension=1, tiled=True
        )
        full_cols = lax.all_gather(lower_group, "row", axis=2, tiled=True)
        masked_rows = full_cols * local_mask[:, :, None].astype(jnp.bfloat16)
        schur_terms = jnp.einsum(
            "gka,gkc->gac", masked_rows, offdiag, preferred_element_type=jnp.float32
        )
        schur_part = lax.psum_scatter(
            schur_terms.astype(jnp.bfloat16), "col", scatter_dimension=1, tiled=True
        ).astype(jnp.float32)
        return (offdiag, inverse_group - schur_part)

    group_size = 4
    turn_count = lower_panels.shape[0] // group_size

    def regroup(source_array):
        return source_array.reshape((turn_count, group_size) + source_array.shape[1:])

    def one_turn(running, inputs_now):
        return (running, solve_group(*inputs_now))

    finished, outputs = lax.scan(
        one_turn,
        jnp.int32(0),
        (
            regroup(lower_panels),
            regroup(struct_blocks),
            regroup(struct_count),
            regroup(diag_inverse),
        ),
    )
    offdiag_all, diag_all = outputs
    return (offdiag_all.reshape(lower_panels.shape), diag_all.reshape(diag_inverse.shape))


def solution(mesh):
    in_specs = (P("col", "row"), P(None, "col", "row"), P(), P(), P(None, "col", "row"))
    out_specs = (P(None, "col", "row"), P(None, "col", "row"))
    return jax.shard_map(body, mesh=mesh, in_specs=in_specs, out_specs=out_specs, check_vma=False)
```

profile of v0, /device:TPU:0, one launch (start us, length us, event | category | flops | bytes accessed | tf_op | source)
XLA Modules:
  0.0 269.8 jit_solution(14597254614823216027)
XLA Ops:
  7.2 0.0 all-gather.4.cloned.1.call-start
  7.2 0.7 all-gather.4.cloned.1.call-update
  7.9 0.0 all-gather.6.cloned.1.call-start
  7.9 0.7 all-gather.6.cloned.1.call-update
  8.6 0.0 all-gather.8.cloned.1.call-start
  8.7 0.7 all-gather.8.cloned.1.call-update
  9.4 0.0 reduce-scatter.3.cloned.1.call-start
  9.4 0.7 iota_compare_fusion.1
  10.2 0.7 fusion.9
  10.9 0.7 compare_convert_fusion
  11.6 0.0 copy-start.1
  11.6 61.3 %all-gather.4.cloned.1.call-done = bf16[4,1536,256]{2,1,0:T(8,128)(2,1)} async-done(((bf16[4,192,256]{2,1,0:T(8,128)(2,1)}), bf16[4,1536,256]{2,1,0:T(8,128)(2,1)}) %all-gather.4.cloned.1.call-update) | async-done | bytes 3145744 | tf_op jit(solution)/shard_map/while/body/eval_jaxpr/all_gather | solution.py:22
  72.9 2.4 broadcast_multiply_fusion
  75.3 0.0 copy-done.1
  75.3 2.0 fusion.2
  77.3 3.5 %copy.10 = bf16[4,16,128,256]{3,2,1,0:T(8,128)(2,1)} copy(bf16[4,16,128,256]{3,1,2,0:T(8,128)(2,1)S(1)} %fusion.2) | data formatting | bytes 8388608 | tf_op jit(solution)/shard_map/while/body/eval_jaxpr/convert_element_type | solution.py:36
  80.9 9.0 %all-gather.6.cloned.1.call-done = bf16[256,2048]{1,0:T(8,128)(2,1)} async-done(((bf16[256,512]{1,0:T(8,128)(2,1)}), bf16[256,2048]{1,0:T(8,128)(2,1)}) %all-gather.6.cloned.1.call-update) | async-done | bytes 1048592 | tf_op jit(solution)/shard_map/all_gather | solution.py:12
  89.9 3.8 %convolution_negate_fusion = f32[4,256,256]{1,2,0:T(8,128)S(1)} fusion(bf16[4,2048,256]{2,1,0:T(8,128)(2,1)} %bitcast.23, bf16[256,2048]{1,0:T(8,128)(2,1)} %all-gather.6.cloned.1.call-done), kind=kOutput, calls=%fused_computation.7 | convolution fusion | flops 1074003968 | bytes 6291456 | tf_op jit(solution)/shard_map/while/body/eval_jaxpr/rw,gwc->grc/dot_general | solution.py:37
  93.7 4.4 %convolution_convert_fusion = bf16[4,12,128,256]{3,1,2,0:T(8,128)(2,1)S(1)} fusion(f32[4,2,128,256]{3,2,1,0:T(8,128)S(1)} %bitcast.24, pred[4,16,12]{2,1,0:T(8,128)(4,1)S(1)} %fusion.9, s32[]{:T(128)S(6)} %select_n.26), kind=kOutput, calls=%fused_computation.3 | convolution fusion | flops 39321600 | bytes 4196356 | tf_op jit(solution)/shard_map/while/body/eval_jaxpr/gjk,gjic->gkic/dot_general | solution.py:45
  98.1 2.9 %copy.12 = bf16[4,12,128,256]{3,2,1,0:T(8,128)(2,1)} copy(bf16[4,12,128,256]{3,1,2,0:T(8,128)(2,1)S(1)} %convolution_convert_fusion) | data formatting | bytes 6291456 | tf_op jit(solution)/shard_map/while/body/eval_jaxpr/convert_element_type | solution.py:54
  101.0 0.0 copy-start.2
  101.0 0.0 reduce-scatter.3.cloned.1.call-update
  101.0 0.0 copy-start
  101.0 0.0 reduce-scatter.5.cloned.1.call-start
  101.1 0.5 copy-done.2
  101.6 0.1 compare_convert_fusion.1
  101.7 9.6 %all-gather.8.cloned.1.call-done = bf16[4,192,1024]{2,1,0:T(8,128)(2,1)} async-done(((bf16[4,192,256]{2,1,0:T(8,128)(2,1)}), bf16[4,192,1024]{2,1,0:T(8,128)(2,1)}) %all-gather.8.cloned.1.call-update) | async-done | bytes 1572880 | tf_op jit(solution)/shard_map/while/body/eval_jaxpr/all_gather | solution.py:56
  111.3 78.3 %reduce-scatter.3.cloned.1.call-done = bf16[4,192,256]{2,1,0:T(8,128)(2,1)} async-done(((bf16[4,1536,256]{2,1,0:T(8,128)(2,1)}), bf16[4,192,256]{2,1,0:T(8,128)(2,1)}) %reduce-scatter.3.cloned.1.call-update) | async-done | bytes 393232 | tf_op jit(solution)/shard_map/while/body/eval_jaxpr/reduce_scatter | solution.py:53
  189.6 3.8 %convolution_convert_fusion.1 = bf16[4,1024,256]{2,1,0:T(8,128)(2,1)} fusion(bf16[4,192,256]{2,1,0:T(8,128)(2,1)} %reduce-scatter.3.cloned.1.call-done, bf16[4,192,1024]{2,1,0:T(8,128)(2,1)} %all-gather.8.cloned.1.call-done, bf16[4,192]{1,0:T(4,128)(2,1)S(1)} %compare_convert_fusion.1), kind=kOutput, calls=%fused_computation.4 | convolution fusion | flops 404488192 | bytes 4064768 | tf_op jit(solution)/shard_map/while/body/eval_jaxpr/gka,gkc->gac/dot_general | solution.py:58
  193.4 0.0 reduce-scatter.5.cloned.1.call-update
  193.5 68.0 %reduce-scatter.5.cloned.1.call-done = bf16[4,128,256]{2,1,0:T(8,128)(2,1)} async-done(((bf16[4,1024,256]{2,1,0:T(8,128)(2,1)}), bf16[4,128,256]{2,1,0:T(8,128)(2,1)}) %reduce-scatter.5.cloned.1.call-update) | async-done | bytes 262160 | tf_op jit(solution)/shard_map/while/body/eval_jaxpr/reduce_scatter | solution.py:61
  261.5 0.0 copy-done
  261.5 1.8 convert_subtract_fusion
  (2 shorter events, 0.0 us)
Async XLA Ops:
  7.2 65.8 %all-gather.4.cloned.1.call-start = ((), (), s32[]{:S(2)}) async-start(), calls=%async_computation.2 | async-start | bytes 3538944 | tf_op jit(solution)/shard_map/while/body/eval_jaxpr/all_gather | solution.py:22
  7.9 82.0 %all-gather.6.cloned.1.call-start = ((), (), s32[]{:S(2)}) async-start(), calls=%async_computation.3 | async-start | bytes 1310720 | tf_op jit(solution)/shard_map/all_gather | solution.py:12
  8.6 102.7 %all-gather.8.cloned.1.call-start = ((), (), s32[]{:S(2)}) async-start(), calls=%async_computation.5 | async-start | bytes 1966080 | tf_op jit(solution)/shard_map/while/body/eval_jaxpr/all_gather | solution.py:56
  9.4 180.2 %reduce-scatter.3.cloned.1.call-start = ((), (), s32[]{:S(2)}) async-start(), calls=%async_computation.4 | async-start | bytes 3538944 | tf_op jit(solution)/shard_map/while/body/eval_jaxpr/reduce_scatter | solution.py:53
  11.6 63.7 %copy-start.1 = (s32[4,12]{1,0:T(4,128)S(1)}, s32[4,12]{1,0:T(4,128)}, u32[]{:S(2)}) copy-start(s32[4,12]{1,0:T(4,128)} %param.7) | copy-start | bytes 580
  101.0 0.7 copy-start.2
  101.0 160.5 %copy-start = (f32[4,128,256]{2,1,0:T(8,128)S(1)}, f32[4,128,256]{2,1,0:T(8,128)}, u32[]{:S(2)}) copy-start(f32[4,128,256]{2,1,0:T(8,128)} %param.9) | copy-start | bytes 1572868
  101.0 160.5 %reduce-scatter.5.cloned.1.call-start = ((), (), s32[]{:S(2)}) async-start(), calls=%async_computation.6 | async-start | bytes 2359296 | tf_op jit(solution)/shard_map/while/body/eval_jaxpr/reduce_scatter | solution.py:61
Sparse Core Ops, SparseCore 0:
  10.2 62.7 all-gather.3
  74.5 15.3 all-gather.5
  91.5 19.8 all-gather.7
  115.3 74.2 reduce-scatter.2
  193.6 67.8 reduce-scatter.4
where the time goes:
time: 270 us
  waiting for transfers between devices  228 us (84%)
  matrix products  14 us (5%)
  between operations  13.8 us (5%)
  local copies, waits for them, and re-layouts  6.97 us (3%)
  other arithmetic  6.43 us (2%)
    reduce_scatter x1, waiting for transfers between devices, solve_group(): lax.psum_scatter(selected.astype(jnp.bfloat16), 'col', scatter_dimension=...  78.3 us
    reduce_scatter x1, waiting for transfers between devices, solve_group(): lax.psum_scatter(schur_terms.astype(jnp.bfloat16), 'col', scatter_dimensi...  68 us
    all_gather x1, waiting for transfers between devices, solve_group(): gathered = lax.all_gather(lower_group, 'col', axis=1, tiled=True)  61.3 us
    all_gather x1, waiting for transfers between devices, solve_group(): full_cols = lax.all_gather(lower_group, 'row', axis=2, tiled=True)  9.62 us
    all_gather x1, waiting for transfers between devices, body(): root_panel = lax.all_gather(root_inverse, 'row', axis=1, tiled=True)  9.03 us
  transfers between devices with their start and end apart: 5, of which 5 were waited for; matrix products, arithmetic and copies ran while one was open for 8% of the time, Pallas kernels for 0%

commit v1 on v0

--- a/solution.py
+++ b/solution.py
@@ -1,6 +1,10 @@
+import functools
+
 import jax
 import jax.numpy as jnp
 from jax import lax
+from jax.experimental import pallas as pl
+from jax.experimental.pallas import tpu as pltpu
 from jax.sharding import PartitionSpec as P
 
 BLOCK = 128
@@ -86,7 +90,306 @@
     return (offdiag_all.reshape(lower_panels.shape), diag_all.reshape(diag_inverse.shape))
 
 
+def place(slices):
+    row, col = lax.axis_index("row"), lax.axis_index("col")
+    return row // 2, row % 2, col // 2, col % 2
+
+
+def at(y, core, z, x):
+    return {"row": 2 * y + core, "col": 2 * z + x}
+
+
+def greet(peers):
+    barrier = pltpu.get_barrier_semaphore()
+    for peer in peers:
+        pl.semaphore_signal(barrier, inc=1, device_id=peer, device_id_type=pl.DeviceIdType.MESH)
+    pl.semaphore_wait(barrier, len(peers))
+
+
+def send(src, dst, send_sem, recv_sem, device):
+    return pltpu.make_async_remote_copy(
+        src_ref=src,
+        dst_ref=dst,
+        send_sem=send_sem,
+        recv_sem=recv_sem,
+        device_id=device,
+        device_id_type=pl.DeviceIdType.MESH,
+    )
+
+
+def gather_kernel(slices, root_ref, panel_ref, half_ref, quad_ref, own_ref, side_ref, *sems):
+    (zr_s, zr_r, zp_s, zp_r, xr_s, xr_r, xp_s, xp_r, yr_s, yr_r, yp_s, yp_r, hc_s, hc_r, qc_s, qc_r, pc_s, pc_r, loc) = sems
+    y, core, z, x = place(slices)
+    width = root_ref.shape[1]
+    chunk = 2 * slices
+    lanes = pl.ds(pl.multiple_of(core * width, width), width)
+    part = side_ref.shape[3]
+    x_peer, y_peer, c_peer = at(y, core, z, 1 - x), at(1 - y, core, z, x), at(y, 1 - core, z, x)
+
+    def z_at(d):
+        return lax.rem(z + d, slices)
+
+    z_peers = [at(y, core, z_at(d), x) for d in range(1, slices)]
+    greet(z_peers + [x_peer, y_peer, c_peer])
+
+    def half_piece(zz, xx):
+        return half_ref.at[lax.rem(2 * zz + xx + slices * y, chunk), :, lanes]
+
+    def quad_piece(zz, xx):
+        return quad_ref.at[2 * lax.rem(zz, slices // 2) + xx, :, lanes]
+
+    def own_piece(zz, xx):
+        return own_ref.at[2 * zz + xx]
+
+    def in_quad(zz):
+        return zz // (slices // 2) == y
+
+    def z_panel(d):
+        return send(panel_ref.at[z_at(d)], own_piece(z, x), zp_s.at[d], zp_r.at[d], at(y, core, z_at(d), x))
+
+    def z_root(d):
+        return send(root_ref, half_piece(z, x), zr_s.at[d], zr_r.at[d], at(y, core, z_at(d), x))
+
+    def back(d):
+        return lax.rem(z + slices - d, slices)
+
+    def x_panel(d):
+        src = panel_ref.at[z] if d == 0 else own_piece(back(d), x)
+        return send(src, own_piece(back(d), x), xp_s.at[d], xp_r.at[d], x_peer)
+
+    def x_root(d):
+        src = root_ref if d == 0 else half_piece(back(d), x)
+        return send(src, half_piece(back(d), x), xr_s.at[d], xr_r.at[d], x_peer)
+
+    def y_root(zz, xx, src):
+        index = 2 * lax.rem(zz, slices // 2) + xx
+        return send(src, quad_ref.at[index, :, lanes], yr_s.at[index], yr_r.at[index], y_peer)
+
+    def c_half(slot, zz, xx, src):
+        return send(src, half_piece(zz, xx), hc_s.at[slot], hc_r.at[slot], c_peer)
+
+    def c_quad(index):
+        return send(quad_ref.at[index, :, lanes], quad_ref.at[index, :, lanes], qc_s.at[index], qc_r.at[index], c_peer)
+
+    my_side = own_ref.at[:, :, pl.ds(pl.multiple_of(x * part, part), part)]
+
+    def side_slot(yy, cc):
+        return side_ref.at[2 * yy + cc]
+
+    y_side = send(my_side, side_slot(y, core), yp_s, yp_r, y_peer)
+    c_side = [
+        send(my_side, side_slot(y, core), pc_s.at[0], pc_r.at[0], c_peer),
+        send(side_slot(1 - y, core), side_slot(1 - y, core), pc_s.at[1], pc_r.at[1], c_peer),
+    ]
+
+    for d in range(1, slices):
+        z_panel(d).start()
+    x_panel(0).start()
+    for d in range(1, slices):
+        z_root(d).start()
+    x_root(0).start()
+
+    @pl.when(in_quad(z))
+    def _():
+        y_root(z, x, root_ref).start()
+
+    c_half(0, z, x, root_ref).start()
+    local = [
+        pltpu.make_async_copy(root_ref, half_piece(z, x), loc.at[0]),
+        pltpu.make_async_copy(panel_ref.at[z], own_piece(z, x), loc.at[1]),
+    ]
+    for copy in local:
+        copy.start()
+    for d in range(1, slices):
+        z_panel(d).wait_recv()
+        x_panel(d).start()
+    local[1].wait()
+    for d in range(slices):
+        x_panel(d).wait_recv()
+    y_side.start()
+    c_side[0].start()
+    own_side = pltpu.make_async_copy(my_side, side_slot(y, core), loc.at[2])
+    own_side.start()
+
+    def spread_on(slot, zz, xx):
+        @pl.when(in_quad(zz))
+        def _():
+            y_root(zz, xx, half_piece(zz, xx)).start()
+
+        c_half(slot, zz, xx, half_piece(zz, xx)).start()
+
+    x_root(0).wait_recv()
+    spread_on(slices, z, 1 - x)
+    for d in range(1, slices):
+        z_root(d).wait_recv()
+        x_root(d).start()
+        spread_on(d, back(d), x)
+    for d in range(1, slices):
+        x_root(d).wait_recv()
+        spread_on(slices + d, back(d), 1 - x)
+    y_side.wait_recv()
+    c_side[1].start()
+    for index in range(slices):
+        send(root_ref, quad_ref.at[index, :, lanes], yr_s.at[index], yr_r.at[index], y_peer).wait_recv()
+        c_quad(index).start()
+    for slot in range(2 * slices):
+        c_half(slot, z, x, root_ref).wait_recv()
+    for index in range(slices):
+        c_quad(index).wait_recv()
+    for copy in c_side:
+        copy.wait_recv()
+    local[0].wait()
+    own_side.wait()
+    for d in range(slices):
+        if d > 0:
+            z_panel(d).wait_send()
+            z_root(d).wait_send()
+        x_panel(d).wait_send()
+        x_root(d).wait_send()
+        send(root_ref, quad_ref.at[d, :, lanes], yr_s.at[d], yr_r.at[d], y_peer).wait_send()
+        c_quad(d).wait_send()
+    for slot in range(2 * slices):
+        c_half(slot, z, x, root_ref).wait_send()
+    y_side.wait_send()
+    for copy in c_side:
+        copy.wait_send()
+
+
+def solve_kernel(list_ref, count_ref, half_ref, quad_ref, own_ref, side_ref, off_ref, schur_ref, spread, product):
+    half = half_ref.shape[0] // 2
+    tile = 2 * BLOCK
+    used = count_ref[0]
+    spread[...] = jnp.zeros_like(spread)
+    for k in range(NSMAX):
+
+        @pl.when(k < used)
+        def _():
+            rows = pl.ds(pl.multiple_of(list_ref[k] * BLOCK, BLOCK), BLOCK)
+            spread[rows, :] = own_ref[pl.ds(k * BLOCK, BLOCK), :]
+
+    near, far = spread[:half, :], spread[half:, :]
+
+    def step(t, carry):
+        rows = pl.ds(pl.multiple_of(t * tile, tile), tile)
+        low = pl.ds(pl.multiple_of(half + t * tile, tile), tile)
+        product[rows, :] = jnp.dot(
+            half_ref[rows, :], near, preferred_element_type=jnp.float32
+        ) + lax.dot_general(
+            half_ref[pl.ds(half, half), rows], far, (((0,), (0,)), ((), ())), preferred_element_type=jnp.float32
+        )
+        product[low, :] = jnp.dot(
+            half_ref[low, :], near, preferred_element_type=jnp.float32
+        ) + jnp.dot(quad_ref[rows, :], far, preferred_element_type=jnp.float32)
+        return carry
+
+    lax.fori_loop(0, half // tile, step, 0)
+    for k in range(NSMAX):
+        rows = pl.ds(pl.multiple_of(list_ref[k] * BLOCK, BLOCK), BLOCK)
+        off_ref[pl.ds(k * BLOCK, BLOCK), :] = jnp.where(k < used, -product[rows, :], 0.0).astype(jnp.bfloat16)
+    off = off_ref[...]
+    for part in range(side_ref.shape[0]):
+        schur_ref[part] = lax.dot_general(
+            side_ref[part], off, (((0,), (0,)), ((), ())), preferred_element_type=jnp.float32
+        ).astype(jnp.bfloat16)
+
+
+def return_kernel(slices, off_ref, schur_ref, off_out, schur_out, os, orr, ss, sr, loc):
+    y, core, z, x = place(slices)
+
+    def target(d):
+        return at(y, core, lax.rem(z + d, slices), x)
+
+    greet([target(d) for d in range(1, slices)])
+    copies = []
+    for d in range(1, slices):
+        zz = lax.rem(z + d, slices)
+        copies.append(send(off_ref.at[2 * zz + x], off_out.at[z], os.at[d], orr.at[d], target(d)))
+    for d in range(1, slices):
+        zz = lax.rem(z + d, slices)
+        copies.append(send(schur_ref.at[zz], schur_out.at[z], ss.at[d], sr.at[d], target(d)))
+    for copy in copies:
+        copy.start()
+    local = [
+        pltpu.make_async_copy(off_ref.at[2 * z + x], off_out.at[z], loc.at[0]),
+        pltpu.make_async_copy(schur_ref.at[z], schur_out.at[z], loc.at[1]),
+    ]
+    for copy in local:
+        copy.start()
+    for copy in local + copies:
+        copy.wait()
+
+
+def owner_body(slices, root_inverse, lower_panels, struct_blocks, struct_count, diag_inverse):
+    y, core, z, x = place(slices)
+    vmem = pl.BlockSpec(memory_space=pltpu.VMEM)
+    smem = pl.BlockSpec(memory_space=pltpu.SMEM)
+    bf16 = jnp.bfloat16
+    root_rows, root_cols = root_inverse.shape
+    count, local_rows, local_cols = lower_panels.shape
+    chunk = 2 * slices
+    order = root_rows * chunk
+    part = local_cols // 2
+    dma = pltpu.SemaphoreType.DMA
+    pair = lambda n: [dma((n,)), dma((n,))]
+    one = [dma, dma]
+    half, quad, own, side = pl.pallas_call(
+        functools.partial(gather_kernel, slices),
+        out_shape=[
+            jax.ShapeDtypeStruct((chunk, root_rows, 2 * root_cols), bf16),
+            jax.ShapeDtypeStruct((slices, root_rows, 2 * root_cols), bf16),
+            jax.ShapeDtypeStruct((chunk, local_rows, local_cols), bf16),
+            jax.ShapeDtypeStruct((4, chunk, local_rows, part), bf16),
+        ],
+        in_specs=[vmem] * 2,
+        out_specs=[vmem] * 4,
+        scratch_shapes=pair(slices) * 4 + pair(slices) + one + pair(2 * slices) + pair(slices) + pair(2) + [dma((3,))],
+        compiler_params=pltpu.CompilerParams(collective_id=0, has_side_effects=True),
+    )(root_inverse, lower_panels)
+    blocks = order // BLOCK
+    mine = lax.dynamic_index_in_dim(struct_blocks, z, 0, keepdims=False)
+    listed = lax.rem(mine + y * (blocks // 2), blocks)
+    used = lax.dynamic_slice_in_dim(struct_count, z, 1, 0)
+    packed = chunk * local_rows
+    off, schur = pl.pallas_call(
+        solve_kernel,
+        out_shape=[
+            jax.ShapeDtypeStruct((packed, local_cols), bf16),
+            jax.ShapeDtypeStruct((4, part, local_cols), bf16),
+        ],
+        in_specs=[smem] * 2 + [vmem] * 4,
+        out_specs=[vmem] * 2,
+        scratch_shapes=[pltpu.VMEM((order, local_cols), bf16), pltpu.VMEM((order, local_cols), jnp.float32)],
+    )(
+        listed,
+        used,
+        half.reshape(order, 2 * root_cols),
+        quad.reshape(order // 2, 2 * root_cols),
+        own.reshape(packed, local_cols),
+        side.reshape(4, packed, part),
+    )
+    offdiag, terms = pl.pallas_call(
+        functools.partial(return_kernel, slices),
+        out_shape=[
+            jax.ShapeDtypeStruct(lower_panels.shape, bf16),
+            jax.ShapeDtypeStruct((count, part, local_cols), bf16),
+        ],
+        in_specs=[vmem] * 2,
+        out_specs=[vmem] * 2,
+        scratch_shapes=pair(slices) * 2 + [dma((2,))],
+        compiler_params=pltpu.CompilerParams(collective_id=1, has_side_effects=True),
+    )(off.reshape(chunk, local_rows, local_cols), schur)
+    return (offdiag, diag_inverse - terms.astype(jnp.float32))
+
+
+def spread_body(*arguments):
+    rows, cols = lax.axis_size("row"), lax.axis_size("col")
+    slices = arguments[1].shape[0]
+    if cols == 2 * slices and rows == 4 and slices == 4:
+        return owner_body(slices, *arguments)
+    return body(*arguments)
+
+
 def solution(mesh):
     in_specs = (P("col", "row"), P(None, "col", "row"), P(), P(), P(None, "col", "row"))
     out_specs = (P(None, "col", "row"), P(None, "col", "row"))
-    return jax.shard_map(body, mesh=mesh, in_specs=in_specs, out_specs=out_specs, check_vma=False)
+    return jax.shard_map(spread_body, mesh=mesh, in_specs=in_specs, out_specs=out_specs, check_vma=False)

time: 270 us -> 103 us (0.38)
  waiting for transfers between devices: 228 us -> 0 us
  Pallas kernels: 0 us -> 95.9 us
  matrix products: 14 us -> 0 us
  between operations: 13.8 us -> 0.69 us
  local copies, waits for them, and re-layouts: 6.97 us -> 3.07 us
  other arithmetic: 6.43 us -> 3 us
    reduce_scatter x2 -> x0, waiting for transfers between devices: 146 us -> none  [the longest x1 78.3 us: solve_group(): lax.psum_scatter(selected.astype(jnp.bfloat16), 'col', scatter_dimension=...]
    pallas_call x0 -> x3, Pallas kernels: none -> 95.9 us  [the longest x1 60.3 us: owner_body(): pl.pallas_call(functools.partial(gather_kernel, slices), out_shape=[jax.S...]
    all_gather x3 -> x0, waiting for transfers between devices: 80 us -> none  [the longest x1 61.3 us: solve_group(): gathered = lax.all_gather(lower_group, 'col', axis=1, tiled=True)]
    dot_general x4 -> x0, matrix products: 14 us -> none  [the longest x1 4.41 us: solve_group(): jnp.einsum('gjk,gjic->gkic', own_select, root_part.reshape(group_size, pe...]
    convert_element_type x2 -> x0, local copies, waits for them, and re-layouts: 6.41 us -> none  [the longest x1 3.54 us: solve_group(): spread.astype(jnp.bfloat16).reshape(group_size, root_width, cols_here)]
  transfers between devices with their start and end apart: 5 -> 0, of which waited for: 5 -> 0; matrix products, arithmetic and copies ran while one was open for 8% -> 0% of each run, Pallas kernels for 0% -> 0%
where the time goes in v1:
time: 103 us
  Pallas kernels  95.9 us (93%)
  local copies, waits for them, and re-layouts  3.07 us (3%)
  other arithmetic  3 us (3%)
    pallas_call x1, Pallas kernels, owner_body(): pl.pallas_call(functools.partial(gather_kernel, slices), out_shape=[jax.S...  60.3 us
    pallas_call x1, Pallas kernels, owner_body(): pl.pallas_call(functools.partial(return_kernel, slices), out_shape=[jax.S...  27 us
    pallas_call x1, Pallas kernels, owner_body(): pl.pallas_call(solve_kernel, out_shape=[jax.ShapeDtypeStruct((packed, loc...  8.66 us

profile of v1, /device:TPU:0, one launch (start us, length us, event | category | flops | bytes accessed | tf_op | source)
XLA Modules:
  0.0 102.7 jit_solution(18197061162849123502)
XLA Ops:
  0.7 1.3 %dynamic_slice.8.count_ref = s32[1]{0:T(128)} dynamic-slice(s32[4]{0:T(128)} %param.8, s32[]{:T(128)S(6)} %select_n.14), dynamic_slice_sizes={1} | dynamic-slice | bytes 12 | tf_op jit(solution)/shard_map/dynamic_slice | solution.py:351
  2.0 1.2 %compare_select_fusion.list_ref = s32[12]{0:T(128)} fusion(s32[4,12]{1,0:T(4,128)} %param.7, s32[]{:T(128)S(6)} %select_n.14, s32[]{:T(128)S(6)} %mul.3), kind=kLoop, calls=%fused_computation.1 | loop fusion | flops 84 | bytes 104 | tf_op jit(solution)/shard_map/rem | solution.py:350
  3.2 60.3 %shard_map.68 = (bf16[8,256,1024]{2,1,0:T(8,128)(2,1)}, bf16[4,256,1024]{2,1,0:T(8,128)(2,1)}, bf16[8,192,256]{2,1,0:T(8,128)(2,1)}, bf16[4,8,192,128]{3,2,1,0:T(8,128)(2,1)}) custom-call(bf16[256,512]{1,0:T(8,128)(2,1)} %root_ref.1, bf16[4,192,256]{2,1,0:T(8,128)(2,1)} %panel_ref.1), custom_call_target="tpu_custom_call" | custom-call | tf_op jit(solution)/shard_map/pallas_call | solution.py:335
  63.4 0.0 copy-start
  63.4 8.7 %shard_map.69 = (bf16[1536,256]{1,0:T(8,128)(2,1)}, bf16[4,128,256]{2,1,0:T(8,128)(2,1)}) custom-call(s32[12]{0:T(128)} %compare_select_fusion.list_ref, s32[1]{0:T(128)} %dynamic_slice.8.count_ref, bf16[2048,1024]{1,0:T(8,128)(2,1)} %bitcast.7, bf16[1024,1024]{1,0:T(8,128)(2,1)} %bitcast.8, bf16[1536,256]{1,0:T(8,128)(2,1)} %bitcast.10, ...), custom_call_target="tpu_custom_call" | custom-call | tf_op jit(solution)/shard_map/pallas_call | solution.py:353
  72.1 27.0 %shard_map.70 = (bf16[4,192,256]{2,1,0:T(8,128)(2,1)}, bf16[4,128,256]{2,1,0:T(8,128)(2,1)}) custom-call(bf16[8,192,256]{2,1,0:T(8,128)(2,1)} %bitcast.11, bf16[4,128,256]{2,1,0:T(8,128)(2,1)} %get-tuple-element.15.schur_ref), custom_call_target="tpu_custom_call" | custom-call | tf_op jit(solution)/shard_map/pallas_call | solution.py:370
  99.1 0.0 copy-done
  99.1 1.8 %convert_subtract_fusion = f32[4,128,256]{2,1,0:T(8,128)} fusion(f32[4,128,256]{2,1,0:T(8,128)S(1)} %copy-done, bf16[4,128,256]{2,1,0:T(8,128)(2,1)} %get-tuple-element.17), kind=kLoop, calls=%fused_computation | loop fusion | flops 262144 | bytes 1310720 | tf_op jit(solution)/shard_map/sub | solution.py:381
  100.9 1.8 %copy.8 = bf16[4,192,256]{2,1,0:T(8,128)(2,1)} copy(bf16[4,192,256]{2,1,0:T(8,128)(2,1)} %get-tuple-element.20) | data formatting | bytes 786432
Async XLA Ops:
  63.4 35.7 %copy-start = (f32[4,128,256]{2,1,0:T(8,128)S(1)}, f32[4,128,256]{2,1,0:T(8,128)}, u32[]{:S(2)}) copy-start(f32[4,128,256]{2,1,0:T(8,128)} %param.9) | copy-start | bytes 1572868

commit v2 on v1

--- a/solution.py
+++ b/solution.py
@@ -117,11 +117,15 @@
     )
 
 
+SUB = 2
+
+
 def gather_kernel(slices, root_ref, panel_ref, half_ref, quad_ref, own_ref, side_ref, *sems):
-    (zr_s, zr_r, zp_s, zp_r, xr_s, xr_r, xp_s, xp_r, yr_s, yr_r, yp_s, yp_r, hc_s, hc_r, qc_s, qc_r, pc_s, pc_r, loc) = sems
+    (zo_s, zr_s, zr_r, zp_s, zp_r, xr_s, xr_r, xp_s, xp_r, yr_s, yr_r, yp_s, yp_r, hc_s, hc_r, qc_s, qc_r, pc_s, pc_r, loc) = sems
     y, core, z, x = place(slices)
-    width = root_ref.shape[1]
+    height, width = root_ref.shape[0] // SUB, root_ref.shape[1]
     chunk = 2 * slices
+    middle = slices // 2
     lanes = pl.ds(pl.multiple_of(core * width, width), width)
     part = side_ref.shape[3]
     x_peer, y_peer, c_peer = at(y, core, z, 1 - x), at(1 - y, core, z, x), at(y, 1 - core, z, x)
@@ -129,47 +133,77 @@
     def z_at(d):
         return lax.rem(z + d, slices)
 
-    z_peers = [at(y, core, z_at(d), x) for d in range(1, slices)]
-    greet(z_peers + [x_peer, y_peer, c_peer])
-
-    def half_piece(zz, xx):
-        return half_ref.at[lax.rem(2 * zz + xx + slices * y, chunk), :, lanes]
-
-    def quad_piece(zz, xx):
-        return quad_ref.at[2 * lax.rem(zz, slices // 2) + xx, :, lanes]
+    def back(d):
+        return lax.rem(z + slices - d, slices)
+
+    greet([at(y, core, z_at(d), x) for d in range(1, slices)] + [x_peer, y_peer, c_peer])
+
+    def rows(s):
+        return pl.ds(s * height, height)
+
+    def root_piece(s):
+        return root_ref.at[rows(s)]
+
+    def half_piece(zz, xx, s):
+        return half_ref.at[lax.rem(2 * zz + xx + slices * y, chunk), rows(s), lanes]
 
     def own_piece(zz, xx):
         return own_ref.at[2 * zz + xx]
 
-    def in_quad(zz):
-        return zz // (slices // 2) == y
+    def z_own(way, s):
+        step = 1 - 2 * way
+        return send(
+            root_piece(s), half_piece(z, x, s), zo_s.at[way * SUB + s], zr_r.at[z * SUB + s], at(y, core, z + step, x)
+        )
+
+    def z_pass(zz, s, step):
+        piece = half_piece(zz, x, s)
+        return send(piece, piece, zr_s.at[zz * SUB + s], zr_r.at[zz * SUB + s], at(y, core, z + step, x))
+
+    def when_passed(zz, action):
+        above = (zz + slices - z) // slices
+
+        @pl.when((above == 0) & (z < slices - 1))
+        def _():
+            action(1)
+
+        @pl.when((above == 1) & (z > 0))
+        def _():
+            action(-1)
+
+    def x_root(zz, s, src=None):
+        piece = half_piece(zz, x, s)
+        return send(piece if src is None else src, piece, xr_s.at[zz * SUB + s], xr_r.at[zz * SUB + s], x_peer)
+
+    def quad_piece(index, s):
+        return quad_ref.at[index, rows(s), lanes]
+
+    def y_root(index, s, src):
+        return send(src, quad_piece(index, s), yr_s.at[index * SUB + s], yr_r.at[index * SUB + s], y_peer)
+
+    def c_half(slot, s, src, dst):
+        return send(src, dst, hc_s.at[slot * SUB + s], hc_r.at[slot * SUB + s], c_peer)
+
+    def c_quad(index, s):
+        piece = quad_piece(index, s)
+        return send(piece, piece, qc_s.at[index * SUB + s], qc_r.at[index * SUB + s], c_peer)
+
+    def spread_on(zz, xx, s, src=None):
+        piece = half_piece(zz, xx, s)
+        src = piece if src is None else src
+
+        @pl.when(zz // middle == y)
+        def _():
+            y_root(2 * lax.rem(zz, middle) + xx, s, src).start()
+
+        c_half(2 * zz + xx, s, src, piece).start()
 
     def z_panel(d):
         return send(panel_ref.at[z_at(d)], own_piece(z, x), zp_s.at[d], zp_r.at[d], at(y, core, z_at(d), x))
-
-    def z_root(d):
-        return send(root_ref, half_piece(z, x), zr_s.at[d], zr_r.at[d], at(y, core, z_at(d), x))
-
-    def back(d):
-        return lax.rem(z + slices - d, slices)
 
     def x_panel(d):
         src = panel_ref.at[z] if d == 0 else own_piece(back(d), x)
         return send(src, own_piece(back(d), x), xp_s.at[d], xp_r.at[d], x_peer)
-
-    def x_root(d):
-        src = root_ref if d == 0 else half_piece(back(d), x)
-        return send(src, half_piece(back(d), x), xr_s.at[d], xr_r.at[d], x_peer)
-
-    def y_root(zz, xx, src):
-        index = 2 * lax.rem(zz, slices // 2) + xx
-        return send(src, quad_ref.at[index, :, lanes], yr_s.at[index], yr_r.at[index], y_peer)
-
-    def c_half(slot, zz, xx, src):
-        return send(src, half_piece(zz, xx), hc_s.at[slot], hc_r.at[slot], c_peer)
-
-    def c_quad(index):
-        return send(quad_ref.at[index, :, lanes], quad_ref.at[index, :, lanes], qc_s.at[index], qc_r.at[index], c_peer)
 
     my_side = own_ref.at[:, :, pl.ds(pl.multiple_of(x * part, part), part)]
 
@@ -185,87 +219,107 @@
     for d in range(1, slices):
         z_panel(d).start()
     x_panel(0).start()
-    for d in range(1, slices):
-        z_root(d).start()
-    x_root(0).start()
-
-    @pl.when(in_quad(z))
-    def _():
-        y_root(z, x, root_ref).start()
-
-    c_half(0, z, x, root_ref).start()
-    local = [
-        pltpu.make_async_copy(root_ref, half_piece(z, x), loc.at[0]),
-        pltpu.make_async_copy(panel_ref.at[z], own_piece(z, x), loc.at[1]),
-    ]
+    for s in range(SUB):
+
+        @pl.when(z < slices - 1)
+        def _():
+            z_own(0, s).start()
+
+        @pl.when(z > 0)
+        def _():
+            z_own(1, s).start()
+
+        x_root(z, s, root_piece(s)).start()
+        spread_on(z, x, s, root_piece(s))
+    local = [pltpu.make_async_copy(root_piece(s), half_piece(z, x, s), loc.at[2 + s]) for s in range(SUB)]
+    local.append(pltpu.make_async_copy(panel_ref.at[z], own_piece(z, x), loc.at[1]))
     for copy in local:
         copy.start()
     for d in range(1, slices):
         z_panel(d).wait_recv()
         x_panel(d).start()
-    local[1].wait()
+    for s in range(SUB):
+        x_root(z, s).wait_recv()
+        spread_on(z, 1 - x, s)
+    local[-1].wait()
     for d in range(slices):
         x_panel(d).wait_recv()
     y_side.start()
     c_side[0].start()
-    own_side = pltpu.make_async_copy(my_side, side_slot(y, core), loc.at[2])
+    own_side = pltpu.make_async_copy(my_side, side_slot(y, core), loc.at[0])
     own_side.start()
 
-    def spread_on(slot, zz, xx):
-        @pl.when(in_quad(zz))
-        def _():
-            y_root(zz, xx, half_piece(zz, xx)).start()
-
-        c_half(slot, zz, xx, half_piece(zz, xx)).start()
-
-    x_root(0).wait_recv()
-    spread_on(slices, z, 1 - x)
-    for d in range(1, slices):
-        z_root(d).wait_recv()
-        x_root(d).start()
-        spread_on(d, back(d), x)
-    for d in range(1, slices):
-        x_root(d).wait_recv()
-        spread_on(slices + d, back(d), 1 - x)
+    upper = z // middle
+    folded = z + upper * (slices - 1 - 2 * z)
+    sources = []
+    for i in range(slices - 1):
+        source = i + (i + slices - folded) // slices
+        sources.append(source + upper * (slices - 1 - 2 * source))
+    for i in range(slices):
+        for s in range(SUB):
+            if i < slices - 1:
+                zz = sources[i]
+                send(root_piece(s), half_piece(zz, x, s), zr_s.at[zz * SUB + s], zr_r.at[zz * SUB + s], x_peer).wait_recv()
+                when_passed(zz, lambda step: z_pass(zz, s, step).start())
+                x_root(zz, s).start()
+                spread_on(zz, x, s)
+            if i > 0:
+                x_root(sources[i - 1], s).wait_recv()
+                spread_on(sources[i - 1], 1 - x, s)
     y_side.wait_recv()
     c_side[1].start()
     for index in range(slices):
-        send(root_ref, quad_ref.at[index, :, lanes], yr_s.at[index], yr_r.at[index], y_peer).wait_recv()
-        c_quad(index).start()
+        for s in range(SUB):
+            y_root(index, s, root_piece(s)).wait_recv()
+            c_quad(index, s).start()
     for slot in range(2 * slices):
-        c_half(slot, z, x, root_ref).wait_recv()
+        for s in range(SUB):
+            c_half(slot, s, root_piece(s), quad_piece(0, s)).wait()
+    for copy in c_side:
+        copy.wait()
     for index in range(slices):
-        c_quad(index).wait_recv()
-    for copy in c_side:
-        copy.wait_recv()
-    local[0].wait()
-    own_side.wait()
+        for s in range(SUB):
+            c_quad(index, s).wait()
+            y_root(index, s, root_piece(s)).wait_send()
+            x_root(index, s).wait_send()
     for d in range(slices):
         if d > 0:
             z_panel(d).wait_send()
-            z_root(d).wait_send()
         x_panel(d).wait_send()
-        x_root(d).wait_send()
-        send(root_ref, quad_ref.at[d, :, lanes], yr_s.at[d], yr_r.at[d], y_peer).wait_send()
-        c_quad(d).wait_send()
-    for slot in range(2 * slices):
-        c_half(slot, z, x, root_ref).wait_send()
+    for s in range(SUB):
+
+        @pl.when(z < slices - 1)
+        def _():
+            z_own(0, s).wait_send()
+
+        @pl.when(z > 0)
+        def _():
+            z_own(1, s).wait_send()
+
+        for zz in sources:
+            when_passed(zz, lambda step: z_pass(zz, s, step).wait_send())
+        local[s].wait()
     y_side.wait_send()
-    for copy in c_side:
-        copy.wait_send()
-
-
-def solve_kernel(list_ref, count_ref, half_ref, quad_ref, own_ref, side_ref, off_ref, schur_ref, spread, product):
+    own_side.wait()
+
+
+def solve_kernel(slices, list_ref, count_ref, half_ref, quad_ref, own_ref, side_ref, off_ref, schur_ref, spread, product):
     half = half_ref.shape[0] // 2
     tile = 2 * BLOCK
-    used = count_ref[0]
+    y, _, z, _ = place(slices)
+    blocks = 2 * half // BLOCK
+    used = count_ref[z]
+
+    def block_rows(k):
+        block = lax.rem(list_ref[z, k] + y * (blocks // 2), blocks)
+        return pl.ds(pl.multiple_of(block * BLOCK, BLOCK), BLOCK)
+
     spread[...] = jnp.zeros_like(spread)
     for k in range(NSMAX):
 
         @pl.when(k < used)
         def _():
-            rows = pl.ds(pl.multiple_of(list_ref[k] * BLOCK, BLOCK), BLOCK)
-            spread[rows, :] = own_ref[pl.ds(k * BLOCK, BLOCK), :]
+            spread[block_rows(k), :] = own_ref[pl.ds(k * BLOCK, BLOCK), :]
 
     near, far = spread[:half, :], spread[half:, :]
 
@@ -284,7 +338,7 @@
 
     lax.fori_loop(0, half // tile, step, 0)
     for k in range(NSMAX):
-        rows = pl.ds(pl.multiple_of(list_ref[k] * BLOCK, BLOCK), BLOCK)
+        rows = block_rows(k)
         off_ref[pl.ds(k * BLOCK, BLOCK), :] = jnp.where(k < used, -product[rows, :], 0.0).astype(jnp.bfloat16)
     off = off_ref[...]
     for part in range(side_ref.shape[0]):
@@ -320,7 +374,6 @@
 
 
 def owner_body(slices, root_inverse, lower_panels, struct_blocks, struct_count, diag_inverse):
-    y, core, z, x = place(slices)
     vmem = pl.BlockSpec(memory_space=pltpu.VMEM)
     smem = pl.BlockSpec(memory_space=pltpu.SMEM)
     bf16 = jnp.bfloat16
@@ -342,16 +395,19 @@
         ],
         in_specs=[vmem] * 2,
         out_specs=[vmem] * 4,
-        scratch_shapes=pair(slices) * 4 + pair(slices) + one + pair(2 * slices) + pair(slices) + pair(2) + [dma((3,))],
+        scratch_shapes=[dma((2 * SUB,))]
+        + (pair(slices * SUB) + pair(slices)) * 2
+        + pair(slices * SUB)
+        + one
+        + pair(2 * slices * SUB)
+        + pair(slices * SUB)
+        + pair(2)
+        + [dma((2 + SUB,))],
         compiler_params=pltpu.CompilerParams(collective_id=0, has_side_effects=True),
     )(root_inverse, lower_panels)
-    blocks = order // BLOCK
-    mine = lax.dynamic_index_in_dim(struct_blocks, z, 0, keepdims=False)
-    listed = lax.rem(mine + y * (blocks // 2), blocks)
-    used = lax.dynamic_slice_in_dim(struct_count, z, 1, 0)
     packed = chunk * local_rows
     off, schur = pl.pallas_call(
-        solve_kernel,
+        functools.partial(solve_kernel, slices),
         out_shape=[
             jax.ShapeDtypeStruct((packed, local_cols), bf16),
             jax.ShapeDtypeStruct((4, part, local_cols), bf16),
@@ -360,8 +416,8 @@
         out_specs=[vmem] * 2,
         scratch_shapes=[pltpu.VMEM((order, local_cols), bf16), pltpu.VMEM((order, local_cols), jnp.float32)],
     )(
-        listed,
-        used,
+        struct_blocks,
+        struct_count,
         half.reshape(order, 2 * root_cols),
         quad.reshape(order // 2, 2 * root_cols),
         own.reshape(packed, local_cols),

time: 103 us -> 91.7 us (0.89)
  Pallas kernels: 95.9 us -> 87.2 us
  local copies, waits for them, and re-layouts: 3.07 us -> 1.77 us
  other arithmetic: 3 us -> 1.8 us
    pallas_call x1, Pallas kernels: 27 us -> 19.3 us  [owner_body(): pl.pallas_call(functools.partial(return_kernel, slices), out_shape=[jax.S...]
    dynamic_slice x1 -> x0, local copies, waits for them, and re-layouts: 1.3 us -> none  [owner_body(): used = lax.dynamic_slice_in_dim(struct_count, z, 1, 0)]
    rem x1 -> x0, other arithmetic: 1.2 us -> none  [owner_body(): listed = lax.rem(mine + y * (blocks // 2), blocks)]
where the time goes in v2:
time: 91.7 us; the launch traced here: 91.4 us
  Pallas kernels  87.2 us (95%)
  other arithmetic  1.8 us (2%)
  local copies, waits for them, and re-layouts  1.77 us (2%)
    pallas_call x1, Pallas kernels, owner_body(): pl.pallas_call(functools.partial(gather_kernel, slices), out_shape=[jax.S...  59.8 us
    pallas_call x1, Pallas kernels, owner_body(): pl.pallas_call(functools.partial(return_kernel, slices), out_shape=[jax.S...  19.3 us
    pallas_call x1, Pallas kernels, owner_body(): pl.pallas_call(functools.partial(solve_kernel, slices), out_shape=[jax.Sh...  8.03 us

profile of v2, /device:TPU:0, one launch (start us, length us, event | category | flops | bytes accessed | tf_op | source)
XLA Modules:
  0.0 91.4 jit_solution(13888297765507450755)
XLA Ops:
  0.6 59.8 %shard_map.68 = (bf16[8,256,1024]{2,1,0:T(8,128)(2,1)}, bf16[4,256,1024]{2,1,0:T(8,128)(2,1)}, bf16[8,192,256]{2,1,0:T(8,128)(2,1)}, bf16[4,8,192,128]{3,2,1,0:T(8,128)(2,1)}) custom-call(bf16[256,512]{1,0:T(8,128)(2,1)} %root_ref.1, bf16[4,192,256]{2,1,0:T(8,128)(2,1)} %panel_ref.1), custom_call_target="tpu_custom_call" | custom-call | tf_op jit(solution)/shard_map/pallas_call | solution.py:388
  60.5 0.0 copy-start
  60.5 8.0 %shard_map.69 = (bf16[1536,256]{1,0:T(8,128)(2,1)}, bf16[4,128,256]{2,1,0:T(8,128)(2,1)}) custom-call(s32[4,12]{1,0:T(4,128)} %list_ref.1, s32[4]{0:T(128)} %count_ref.1, bf16[2048,1024]{1,0:T(8,128)(2,1)} %bitcast.5, bf16[1024,1024]{1,0:T(8,128)(2,1)} %bitcast.6, bf16[1536,256]{1,0:T(8,128)(2,1)} %bitcast.8, bf16[4,1536,128]{2,1,0:T(8,128)(2,1)} %bitcast.7), custom_call_target="tpu_custom_call" | custom-call | tf_op jit(solution)/shard_map/pallas_call | solution.py:409
  68.5 19.3 %shard_map.70 = (bf16[4,192,256]{2,1,0:T(8,128)(2,1)}, bf16[4,128,256]{2,1,0:T(8,128)(2,1)}) custom-call(bf16[8,192,256]{2,1,0:T(8,128)(2,1)} %bitcast.9, bf16[4,128,256]{2,1,0:T(8,128)(2,1)} %get-tuple-element.15.schur_ref), custom_call_target="tpu_custom_call" | custom-call | tf_op jit(solution)/shard_map/pallas_call | solution.py:426
  87.9 0.0 copy-done
  87.9 1.8 %convert_subtract_fusion = f32[4,128,256]{2,1,0:T(8,128)} fusion(f32[4,128,256]{2,1,0:T(8,128)S(1)} %copy-done, bf16[4,128,256]{2,1,0:T(8,128)(2,1)} %get-tuple-element.17), kind=kLoop, calls=%fused_computation | loop fusion | flops 262144 | bytes 1310720 | tf_op jit(solution)/shard_map/sub | solution.py:437
  89.7 1.8 %copy.8 = bf16[4,192,256]{2,1,0:T(8,128)(2,1)} copy(bf16[4,192,256]{2,1,0:T(8,128)(2,1)} %get-tuple-element.20) | data formatting | bytes 786432
Async XLA Ops:
  60.5 27.4 %copy-start = (f32[4,128,256]{2,1,0:T(8,128)S(1)}, f32[4,128,256]{2,1,0:T(8,128)}, u32[]{:S(2)}) copy-start(f32[4,128,256]{2,1,0:T(8,128)} %param.9) | copy-start | bytes 1572868

commit v3 on v2

--- a/solution.py
+++ b/solution.py
@@ -382,6 +382,7 @@
     chunk = 2 * slices
     order = root_rows * chunk
     part = local_cols // 2
+    grant = 24 * 2**20
     dma = pltpu.SemaphoreType.DMA
     pair = lambda n: [dma((n,)), dma((n,))]
     one = [dma, dma]
@@ -403,7 +404,7 @@
         + pair(slices * SUB)
         + pair(2)
         + [dma((2 + SUB,))],
-        compiler_params=pltpu.CompilerParams(collective_id=0, has_side_effects=True),
+        compiler_params=pltpu.CompilerParams(collective_id=0, has_side_effects=True, vmem_limit_bytes=grant),
     )(root_inverse, lower_panels)
     packed = chunk * local_rows
     off, schur = pl.pallas_call(
@@ -415,6 +416,7 @@
         in_specs=[smem] * 2 + [vmem] * 4,
         out_specs=[vmem] * 2,
         scratch_shapes=[pltpu.VMEM((order, local_cols), bf16), pltpu.VMEM((order, local_cols), jnp.float32)],
+        compiler_params=pltpu.CompilerParams(vmem_limit_bytes=grant),
     )(
         struct_blocks,
         struct_count,
@@ -432,7 +434,7 @@
         in_specs=[vmem] * 2,
         out_specs=[vmem] * 2,
         scratch_shapes=pair(slices) * 2 + [dma((2,))],
-        compiler_params=pltpu.CompilerParams(collective_id=1, has_side_effects=True),
+        compiler_params=pltpu.CompilerParams(collective_id=1, has_side_effects=True, vmem_limit_bytes=grant),
     )(off.reshape(chunk, local_rows, local_cols), schur)
     return (offdiag, diag_inverse - terms.astype(jnp.float32))
 

time: 91.7 us -> 83 us (0.905)
  Pallas kernels: 87.2 us -> 77.2 us
  local copies, waits for them, and re-layouts: 1.77 us -> 4.02 us
  other arithmetic: 1.8 us -> 0.85 us
    pallas_call x1, Pallas kernels: 59.8 us -> 55.4 us  [owner_body(): pl.pallas_call(functools.partial(gather_kernel, slices), out_shape=[jax.S...]
    pallas_call x1, Pallas kernels: 8.03 us -> 4.38 us  [owner_body(): pl.pallas_call(functools.partial(solve_kernel, slices), out_shape=[jax.Sh...]
    unnamed x3 -> x11, local copies, waits for them, and re-layouts: 1.77 us -> 4.02 us
    pallas_call x1, Pallas kernels: 19.3 us -> 17.4 us  [owner_body(): pl.pallas_call(functools.partial(return_kernel, slices), out_shape=[jax.S...]
    sub x1, other arithmetic: 1.8 us -> 0.85 us  [owner_body(): return (offdiag, diag_inverse - terms.astype(jnp.float32))]
where the time goes in v3:
time: 83 us; the launch traced here: 82.7 us
  Pallas kernels  77.2 us (93%)
  local copies, waits for them, and re-layouts  4.02 us (5%)
  other arithmetic  0.85 us (1%)
    pallas_call x1, Pallas kernels, owner_body(): pl.pallas_call(functools.partial(gather_kernel, slices), out_shape=[jax.S...  55.4 us
    pallas_call x1, Pallas kernels, owner_body(): pl.pallas_call(functools.partial(return_kernel, slices), out_shape=[jax.S...  17.4 us
    pallas_call x1, Pallas kernels, owner_body(): pl.pallas_call(functools.partial(solve_kernel, slices), out_shape=[jax.Sh...  4.38 us
    unnamed x11, local copies, waits for them, and re-layouts  4.02 us

profile of v3, /device:TPU:0, one launch (start us, length us, event | category | flops | bytes accessed | tf_op | source)
XLA Modules:
  0.0 82.7 jit_solution(6024789338497252370)
XLA Ops:
  0.6 0.0 copy-start
  0.6 1.0 %copy-done = bf16[4,192,256]{2,1,0:T(8,128)(2,1)S(1)} copy-done((bf16[4,192,256]{2,1,0:T(8,128)(2,1)S(1)}, bf16[4,192,256]{2,1,0:T(8,128)(2,1)}, u32[]{:S(2)}) %copy-start) | copy-done | bytes 393240
  1.6 0.0 copy-start.1
  1.6 0.9 %copy-done.1 = bf16[256,512]{1,0:T(8,128)(2,1)S(1)} copy-done((bf16[256,512]{1,0:T(8,128)(2,1)S(1)}, bf16[256,512]{1,0:T(8,128)(2,1)}, u32[]{:S(2)}) %copy-start.1) | copy-done | bytes 262168
  2.6 55.4 %shard_map.68 = (bf16[8,256,1024]{2,1,0:T(8,128)(2,1)S(1)}, bf16[4,256,1024]{2,1,0:T(8,128)(2,1)S(1)}, bf16[8,192,256]{2,1,0:T(8,128)(2,1)S(1)}, bf16[4,8,192,128]{3,2,1,0:T(8,128)(2,1)S(1)}) custom-call(bf16[256,512]{1,0:T(8,128)(2,1)S(1)} %copy-done.1, bf16[4,192,256]{2,1,0:T(8,128)(2,1)S(1)} %copy-done), custom_call_target="tpu_custom_call" | custom-call | tf_op jit(solution)/shard_map/pallas_call | solution.py:389
  58.0 0.0 copy-start.2
  58.0 0.7 copy-done.2
  58.7 0.0 copy-start.3
  58.7 0.7 copy-done.3
  59.3 0.0 copy-start.4
  59.3 4.4 %shard_map.69 = (bf16[1536,256]{1,0:T(8,128)(2,1)S(1)}, bf16[4,128,256]{2,1,0:T(8,128)(2,1)S(1)}) custom-call(s32[4,12]{1,0:T(4,128)S(1)} %copy-done.2, s32[4]{0:T(128)S(1)} %copy-done.3, bf16[2048,1024]{1,0:T(8,128)(2,1)S(1)} %bitcast.5, bf16[1024,1024]{1,0:T(8,128)(2,1)S(1)} %bitcast.6, bf16[1536,256]{1,0:T(8,128)(2,1)S(1)} %bitcast.8, ...), custom_call_target="tpu_custom_call" | custom-call | tf_op jit(solution)/shard_map/pallas_call | solution.py:410
  63.7 17.4 %shard_map.70 = (bf16[4,192,256]{2,1,0:T(8,128)(2,1)S(1)}, bf16[4,128,256]{2,1,0:T(8,128)(2,1)S(1)}) custom-call(bf16[8,192,256]{2,1,0:T(8,128)(2,1)S(1)} %bitcast.9, bf16[4,128,256]{2,1,0:T(8,128)(2,1)S(1)} %get-tuple-element.15.schur_ref), custom_call_target="tpu_custom_call" | custom-call | tf_op jit(solution)/shard_map/pallas_call | solution.py:428
  81.1 0.0 copy-done.4
  81.1 0.8 %convert_subtract_fusion = f32[4,128,256]{2,1,0:T(8,128)} fusion(f32[4,128,256]{2,1,0:T(8,128)S(1)} %copy-done.4, bf16[4,128,256]{2,1,0:T(8,128)(2,1)S(1)} %get-tuple-element.17), kind=kLoop, calls=%fused_computation | loop fusion | flops 262144 | bytes 1310720 | tf_op jit(solution)/shard_map/sub | solution.py:439
  82.0 0.7 copy.8
Async XLA Ops:
  0.6 1.0 %copy-start = (bf16[4,192,256]{2,1,0:T(8,128)(2,1)S(1)}, bf16[4,192,256]{2,1,0:T(8,128)(2,1)}, u32[]{:S(2)}) copy-start(bf16[4,192,256]{2,1,0:T(8,128)(2,1)} %panel_ref.1) | copy-start | bytes 1179652
  1.6 0.9 %copy-start.1 = (bf16[256,512]{1,0:T(8,128)(2,1)S(1)}, bf16[256,512]{1,0:T(8,128)(2,1)}, u32[]{:S(2)}) copy-start(bf16[256,512]{1,0:T(8,128)(2,1)} %root_ref.1) | copy-start | bytes 786436
  58.0 0.7 copy-start.2
  58.7 0.7 copy-start.3
  59.3 21.8 %copy-start.4 = (f32[4,128,256]{2,1,0:T(8,128)S(1)}, f32[4,128,256]{2,1,0:T(8,128)}, u32[]{:S(2)}) copy-start(f32[4,128,256]{2,1,0:T(8,128)} %param.9) | copy-start | bytes 1572868

commit v4 on v3

--- a/solution.py
+++ b/solution.py
@@ -216,31 +216,31 @@
         send(side_slot(1 - y, core), side_slot(1 - y, core), pc_s.at[1], pc_r.at[1], c_peer),
     ]
 
+    for s in range(SUB):
+
+        @pl.when(z < slices - 1)
+        def _():
+            z_own(0, s).start()
+
+        @pl.when(z > 0)
+        def _():
+            z_own(1, s).start()
+
+        x_root(z, s, root_piece(s)).start()
+        spread_on(z, x, s, root_piece(s))
     for d in range(1, slices):
         z_panel(d).start()
     x_panel(0).start()
-    for s in range(SUB):
-
-        @pl.when(z < slices - 1)
-        def _():
-            z_own(0, s).start()
-
-        @pl.when(z > 0)
-        def _():
-            z_own(1, s).start()
-
-        x_root(z, s, root_piece(s)).start()
-        spread_on(z, x, s, root_piece(s))
     local = [pltpu.make_async_copy(root_piece(s), half_piece(z, x, s), loc.at[2 + s]) for s in range(SUB)]
     local.append(pltpu.make_async_copy(panel_ref.at[z], own_piece(z, x), loc.at[1]))
     for copy in local:
         copy.start()
+    for s in range(SUB):
+        x_root(z, s).wait_recv()
+        spread_on(z, 1 - x, s)
     for d in range(1, slices):
         z_panel(d).wait_recv()
         x_panel(d).start()
-    for s in range(SUB):
-        x_root(z, s).wait_recv()
-        spread_on(z, 1 - x, s)
     local[-1].wait()
     for d in range(slices):
         x_panel(d).wait_recv()

time: 83 us -> 84.3 us (1.016)
  Pallas kernels: 77.2 us -> 78.6 us
    pallas_call x1, Pallas kernels: 55.4 us -> 56.6 us  [owner_body(): pl.pallas_call(functools.partial(gather_kernel, slices), out_shape=[jax.S...]
where the time goes in v4:
time: 84.3 us; the launch traced here: 84.1 us
  Pallas kernels  78.6 us (93%)
  local copies, waits for them, and re-layouts  4.02 us (5%)
  other arithmetic  0.85 us (1%)
    pallas_call x1, Pallas kernels, owner_body(): pl.pallas_call(functools.partial(gather_kernel, slices), out_shape=[jax.S...  56.6 us
    pallas_call x1, Pallas kernels, owner_body(): pl.pallas_call(functools.partial(return_kernel, slices), out_shape=[jax.S...  17.5 us
    pallas_call x1, Pallas kernels, owner_body(): pl.pallas_call(functools.partial(solve_kernel, slices), out_shape=[jax.Sh...  4.45 us
    unnamed x11, local copies, waits for them, and re-layouts  4.02 us

profile of v4, /device:TPU:0, one launch (start us, length us, event | category | flops | bytes accessed | tf_op | source)
XLA Modules:
  0.0 84.1 jit_solution(840605280655934878)
XLA Ops:
  0.6 0.0 copy-start
  0.6 1.0 %copy-done = bf16[4,192,256]{2,1,0:T(8,128)(2,1)S(1)} copy-done((bf16[4,192,256]{2,1,0:T(8,128)(2,1)S(1)}, bf16[4,192,256]{2,1,0:T(8,128)(2,1)}, u32[]{:S(2)}) %copy-start) | copy-done | bytes 393240
  1.6 0.0 copy-start.1
  1.6 0.9 %copy-done.1 = bf16[256,512]{1,0:T(8,128)(2,1)S(1)} copy-done((bf16[256,512]{1,0:T(8,128)(2,1)S(1)}, bf16[256,512]{1,0:T(8,128)(2,1)}, u32[]{:S(2)}) %copy-start.1) | copy-done | bytes 262168
  2.6 56.6 %shard_map.68 = (bf16[8,256,1024]{2,1,0:T(8,128)(2,1)S(1)}, bf16[4,256,1024]{2,1,0:T(8,128)(2,1)S(1)}, bf16[8,192,256]{2,1,0:T(8,128)(2,1)S(1)}, bf16[4,8,192,128]{3,2,1,0:T(8,128)(2,1)S(1)}) custom-call(bf16[256,512]{1,0:T(8,128)(2,1)S(1)} %copy-done.1, bf16[4,192,256]{2,1,0:T(8,128)(2,1)S(1)} %copy-done), custom_call_target="tpu_custom_call" | custom-call | tf_op jit(solution)/shard_map/pallas_call | solution.py:389
  59.2 0.0 copy-start.2
  59.2 0.7 copy-done.2
  59.9 0.0 copy-start.3
  59.9 0.7 copy-done.3
  60.6 0.0 copy-start.4
  60.6 4.4 %shard_map.69 = (bf16[1536,256]{1,0:T(8,128)(2,1)S(1)}, bf16[4,128,256]{2,1,0:T(8,128)(2,1)S(1)}) custom-call(s32[4,12]{1,0:T(4,128)S(1)} %copy-done.2, s32[4]{0:T(128)S(1)} %copy-done.3, bf16[2048,1024]{1,0:T(8,128)(2,1)S(1)} %bitcast.5, bf16[1024,1024]{1,0:T(8,128)(2,1)S(1)} %bitcast.6, bf16[1536,256]{1,0:T(8,128)(2,1)S(1)} %bitcast.8, ...), custom_call_target="tpu_custom_call" | custom-call | tf_op jit(solution)/shard_map/pallas_call | solution.py:410
  65.0 17.5 %shard_map.70 = (bf16[4,192,256]{2,1,0:T(8,128)(2,1)S(1)}, bf16[4,128,256]{2,1,0:T(8,128)(2,1)S(1)}) custom-call(bf16[8,192,256]{2,1,0:T(8,128)(2,1)S(1)} %bitcast.9, bf16[4,128,256]{2,1,0:T(8,128)(2,1)S(1)} %get-tuple-element.15.schur_ref), custom_call_target="tpu_custom_call" | custom-call | tf_op jit(solution)/shard_map/pallas_call | solution.py:428
  82.5 0.0 copy-done.4
  82.5 0.8 %convert_subtract_fusion = f32[4,128,256]{2,1,0:T(8,128)} fusion(f32[4,128,256]{2,1,0:T(8,128)S(1)} %copy-done.4, bf16[4,128,256]{2,1,0:T(8,128)(2,1)S(1)} %get-tuple-element.17), kind=kLoop, calls=%fused_computation | loop fusion | flops 262144 | bytes 1310720 | tf_op jit(solution)/shard_map/sub | solution.py:439
  83.4 0.7 copy.8
Async XLA Ops:
  0.6 1.0 %copy-start = (bf16[4,192,256]{2,1,0:T(8,128)(2,1)S(1)}, bf16[4,192,256]{2,1,0:T(8,128)(2,1)}, u32[]{:S(2)}) copy-start(bf16[4,192,256]{2,1,0:T(8,128)(2,1)} %panel_ref.1) | copy-start | bytes 1179652
  1.6 0.9 %copy-start.1 = (bf16[256,512]{1,0:T(8,128)(2,1)S(1)}, bf16[256,512]{1,0:T(8,128)(2,1)}, u32[]{:S(2)}) copy-start(bf16[256,512]{1,0:T(8,128)(2,1)} %root_ref.1) | copy-start | bytes 786436
  59.2 0.7 copy-start.2
  59.9 0.7 copy-start.3
  60.6 21.9 %copy-start.4 = (f32[4,128,256]{2,1,0:T(8,128)S(1)}, f32[4,128,256]{2,1,0:T(8,128)}, u32[]{:S(2)}) copy-start(f32[4,128,256]{2,1,0:T(8,128)} %param.9) | copy-start | bytes 1572868
